TPU v7x, 32 devices: a whole 2x2x4 slice. The times are simulated.
32 devices in a mesh: row: 4 (over y, x), col: 8 (over z, core).
Axes of the slice: x: 2, y: 2, z: 4, core: 2. Of those that a mesh axis runs over, the one named last changes fastest.
Arguments:
- density: bfloat16 [2048, 2048], P('row', 'col'), may hold values from -0.125 to 0.125
- density_mask: int32 [16, 16], P('row', 'col'), may hold values from 0 to 1, as said below
- response: bfloat16 [2, 2048, 2048], P(None, 'row', 'col'), may hold values from -6 to 6
- response_mask: int32 [2, 16, 16], P(None, 'row', 'col'), may hold values from 0 to 1, as said below
- filter_mask: int32 [16, 16], P('row', 'col'), may hold values from 0 to 1, as said below
Outputs:
- product: bfloat16 [2, 2048, 2048], P(None, 'row', 'col')
Inputs may be any that keep to these rules, and one draw needn't show every extreme that they name: `density_mask`: diagonal blocks are always nonzero; blocks within cyclic block distance 2 of the diagonal are more often nonzero than blocks further out; whole block rows and whole block columns may be nonzero. `response_mask`: for each direction, diagonal blocks are always nonzero; blocks within cyclic block distance 2 of the diagonal are more often nonzero than blocks further out; whole block rows and whole block columns may be nonzero. `filter_mask`: diagonal blocks are always kept; blocks within cyclic block distance 2 * 2 of the diagonal are more often kept than blocks further out; whole block rows and whole block columns may be kept.
All inputs are finite; a program needn't handle non-finite values.
Results may differ from a plain program's by a relative error of at most 0.001.
Values may be sent and summed in bfloat16 or wider, within the bound.
A program may use at most 128 MiB of HBM per device.

v0:
```python
import jax
import jax.numpy as jnp
from jax import lax
from jax.sharding import PartitionSpec as P


def expand_blocks(values, mask, blocksize):
    lead = values.shape[:-2]
    height = values.shape[-2] // blocksize
    width = values.shape[-1] // blocksize
    shaped = values.reshape(lead + (height, blocksize, width, blocksize))
    scaled = shaped * mask.astype(values.dtype)[..., :, None, :, None]
    return scaled.reshape(values.shape)


def body(density, density_mask, response, response_mask, filter_mask):
    blocksize = density.shape[1] // density_mask.shape[1]
    masked_density = expand_blocks(density, density_mask, blocksize)
    masked_response = expand_blocks(response, response_mask, blocksize)
    density_full = lax.all_gather(masked_density, "col", axis=1, tiled=True)
    result = jnp.einsum(
        "ik,dkj->dij",
        density_full,
        lax.all_gather(masked_response, "row", axis=1, tiled=True),
        preferred_element_type=jnp.float32,
    )
    return expand_blocks(result, filter_mask, blocksize).astype(jnp.bfloat16)


def solution(mesh):
    in_specs = (
        P("row", "col"),
        P("row", "col"),
        P(None, "row", "col"),
        P(None, "row", "col"),
        P("row", "col"),
    )
    out_specs = P(None, "row", "col")
    return jax.shard_map(body, mesh=mesh, in_specs=in_specs, out_specs=out_specs, check_vma=False)
```

profile of v0, /device:TPU:9, one launch (start us, length us, event | category | flops | bytes accessed | tf_op | source)
XLA Modules:
  0.0 92.0 jit_solution(6940822390799597102)
XLA Ops:
  6.5 0.0 all-gather.3.cloned.1.call-start
  6.5 0.7 convert_element_type.12
  7.2 0.2 mul.35
  7.4 0.0 copy-start.2
  7.4 0.0 copy-start
  7.5 0.2 mul.36
  7.7 0.0 copy-start.1
  7.7 1.3 %copy.6 = bf16[2,512,256]{1,2,0:T(8,128)(2,1)S(1)} copy(bf16[2,512,256]{2,1,0:T(8,128)(2,1)} %param.7) | data formatting | bytes 1048576 | tf_op args[2]
  8.9 0.9 %mul.37 = bf16[2,512,256]{1,2,0:T(8,128)(2,1)} multiply(bf16[2,512,256]{1,2,0:T(8,128)(2,1)S(1)} %copy.6, bf16[2,512,256]{1,2,0:T(8,128)(2,1)S(1)} %mul.36) | non-fusion elementwise | flops 262144 | bytes 1572864 | tf_op jit(solution)/shard_map/mul | solution.py:12
  9.9 0.0 all-gather.3.cloned.1.call-update
  9.9 0.0 all-gather.5.cloned.1.call-start
  9.9 0.0 copy-done.2
  10.0 0.1 copy.7
  10.1 0.2 mul.38
  10.3 0.0 copy-done
  10.3 0.8 bitcast_multiply_fusion
  11.0 0.0 all-gather.5.cloned.1.call-update
  11.1 0.0 copy-done.1
  11.1 0.1 mul.41
  11.3 34.8 %all-gather.3.cloned.1.call-done = bf16[2,2048,256]{1,2,0:T(8,128)(2,1)} async-done(((bf16[2,512,256]{1,2,0:T(8,128)(2,1)}), bf16[2,2048,256]{1,2,0:T(8,128)(2,1)}) %all-gather.3.cloned.1.call-update) | async-done | bytes 2097168 | tf_op jit(solution)/shard_map/all_gather | solution.py:24
  46.1 34.6 %all-gather.5.cloned.1.call-done = bf16[512,2048]{1,0:T(8,128)(2,1)} async-done(((bf16[512,256]{1,0:T(8,128)(2,1)}), bf16[512,2048]{1,0:T(8,128)(2,1)}) %all-gather.5.cloned.1.call-update) | async-done | bytes 2097168 | tf_op jit(solution)/shard_map/all_gather | solution.py:20
  80.6 3.5 %fusion.8 = bf16[2,512,256]{1,2,0:T(8,128)(2,1)S(1)} fusion(bf16[2,2048,256]{1,2,0:T(8,128)(2,1)} %all-gather.3.cloned.1.call-done, bf16[512,2048]{1,0:T(8,128)(2,1)} %all-gather.5.cloned.1.call-done, f32[512,256]{0,1:T(8,128)S(1)} %bitcast.31), kind=kOutput, calls=%fused_computation.4 | convolution fusion | flops 1074266112 | bytes 5242880 | tf_op jit(solution)/shard_map/ik,dkj->dij/dot_general | solution.py:21
  84.2 1.0 %copy.8 = bf16[2,512,256]{2,1,0:T(8,128)(2,1)} copy(bf16[2,512,256]{1,2,0:T(8,128)(2,1)S(1)} %fusion.8) | data formatting | bytes 1048576 | tf_op jit(solution)/shard_map/convert_element_type | solution.py:27
  (3 shorter events, 0.0 us)
Async XLA Ops:
  6.5 39.5 %all-gather.3.cloned.1.call-start = ((), (), s32[]{:S(2)}) async-start(), calls=%async_computation | async-start | bytes 2621440 | tf_op jit(solution)/shard_map/all_gather | solution.py:24
  7.4 2.5 %copy-start.2 = (s32[4,2]{0,1:T(2,128)S(1)}, s32[4,2]{0,1:T(2,128)}, u32[]{:S(2)}) copy-start(s32[4,2]{0,1:T(2,128)} %param.6) | copy-start | bytes 100
  7.4 2.8 %copy-start = (bf16[512,256]{1,0:T(8,128)(2,1)S(1)}, bf16[512,256]{1,0:T(8,128)(2,1)}, u32[]{:S(2)}) copy-start(bf16[512,256]{1,0:T(8,128)(2,1)} %param.5) | copy-start | bytes 786436
  7.7 3.4 %copy-start.1 = (s32[4,2]{0,1:T(2,128)S(1)}, s32[4,2]{0,1:T(2,128)}, u32[]{:S(2)}) copy-start(s32[4,2]{0,1:T(2,128)} %param.9) | copy-start | bytes 100
  9.9 70.8 %all-gather.5.cloned.1.call-start = ((), (), s32[]{:S(2)}) async-start(), calls=%async_computation.1 | async-start | bytes 2359296 | tf_op jit(solution)/shard_map/all_gather | solution.py:20
Sparse Core Ops, SparseCore 0:
  10.0 36.0 all-gather.2
  47.7 32.9 all-gather.4
where the time goes:
time: 92.2 us; the launch traced here: 92 us
  waiting for transfers between devices  69.4 us (75%)
  between operations  13.5 us (15%)
  matrix products  3.5 us (4%)
  local copies, waits for them, and re-layouts  3.17 us (3%)
  other arithmetic  2.37 us (3%)
    all_gather x1, waiting for transfers between devices, body(): lax.all_gather(masked_response, 'row', axis=1, tiled=True)  34.8 us
    all_gather x1, waiting for transfers between devices, body(): density_full = lax.all_gather(masked_density, 'col', axis=1, tiled=True)  34.6 us
    dot_general x1, matrix products, body(): jnp.einsum('ik,dkj->dij', density_full, lax.all_gather(masked_response, '...  3.5 us
  transfers between devices with their start and end apart: 2, of which 2 were waited for; matrix products, arithmetic and copies ran while one was open for 1% of the time, Pallas kernels for 0%

commit v1 on v0

--- a/solution.py
+++ b/solution.py
@@ -2,6 +2,22 @@
 import jax.numpy as jnp
 from jax import lax
 from jax.sharding import PartitionSpec as P
+
+
+def ring_product(value, axis, dim, term):
+    size, here, span = (lax.axis_size(axis), lax.axis_index(axis), value.shape[dim])
+    forward = [(i, (i + 1) % size) for i in range(size)]
+    left = [(i, (i - 1) % size) for i in range(size)]
+    half = size // 2
+    from_left = from_right = value
+    total = term(value, here * span)
+    for turn in range(1, half + 1):
+        from_left = lax.ppermute(from_left, axis, forward)
+        if turn < size - half:
+            from_right = lax.ppermute(from_right, axis, left)
+            total = total + term(from_right, (here + turn) % size * span)
+        total = total + term(from_left, (here - turn) % size * span)
+    return total
 
 
 def expand_blocks(values, mask, blocksize):
@@ -18,11 +34,16 @@
     masked_density = expand_blocks(density, density_mask, blocksize)
     masked_response = expand_blocks(response, response_mask, blocksize)
     density_full = lax.all_gather(masked_density, "col", axis=1, tiled=True)
-    result = jnp.einsum(
-        "ik,dkj->dij",
-        density_full,
-        lax.all_gather(masked_response, "row", axis=1, tiled=True),
-        preferred_element_type=jnp.float32,
+    result = ring_product(
+        masked_response,
+        "row",
+        1,
+        lambda part, offset: jnp.einsum(
+            "ik,dkj->dij",
+            lax.dynamic_slice_in_dim(density_full, offset, part.shape[1], axis=1),
+            part,
+            preferred_element_type=jnp.float32,
+        ),
     )
     return expand_blocks(result, filter_mask, blocksize).astype(jnp.bfloat16)
 

time: 92.2 us -> 57.7 us (0.63)
  the two profiles are of different devices: /device:TPU:9 before, /device:TPU:0 now
where the time goes in v1:
time: 57.7 us; the launch traced here: 57.5 us
  waiting for transfers between devices  30.4 us (53%)
  between operations  13.5 us (23%)
  starting transfers between devices  5.11 us (9%)
  other arithmetic  3.26 us (6%)
  matrix products  3.08 us (5%)
  local copies, waits for them, and re-layouts  2.19 us (4%)
    ppermute x2, waiting for transfers between devices, ring_product(): from_left = lax.ppermute(from_left, axis, forward)  16.1 us
    all_gather x1, waiting for transfers between devices, body(): density_full = lax.all_gather(masked_density, 'col', axis=1, tiled=True)  14.2 us
    ppermute x2, starting transfers between devices, ring_product(): from_left = lax.ppermute(from_left, axis, forward)  4.08 us
    dot_general x4, matrix products, body(): jnp.einsum('ik,dkj->dij', lax.dynamic_slice_in_dim(density_full, offset,...  3.08 us
    mul x2, other arithmetic, expand_blocks(): scaled = shaped * mask.astype(values.dtype)[..., :, None, :, None]  1.83 us
    convert_element_type x3, other arithmetic, expand_blocks(): scaled = shaped * mask.astype(values.dtype)[..., :, None, :, None]  1.43 us
  transfers between devices with their start and end apart: 4, of which 3 were waited for; matrix products, arithmetic and copies ran while one was open for 7% of the time, Pallas kernels for 0%

profile of v1, /device:TPU:0, one launch (start us, length us, event | category | flops | bytes accessed | tf_op | source)
XLA Modules:
  0.0 57.5 jit_solution(16628742426379531216)
XLA Ops:
  6.5 0.0 copy-start.1
  6.5 0.0 all-gather.2.cloned.1.call-start
  6.5 0.7 %convert_element_type.13 = bf16[4,2]{0,1:T(2,128)(2,1)S(1)} convert(s32[4,2]{0,1:T(2,128)} %param.6) | non-fusion elementwise | flops 8 | bytes 48 | tf_op jit(solution)/shard_map/convert_element_type | solution.py:28
  7.3 0.1 copy.7
  7.4 0.2 mul.50
  7.6 1.7 %bitcast_multiply_fusion = bf16[512,256]{1,0:T(8,128)(2,1)} fusion(bf16[512,256]{1,0:T(8,128)(2,1)} %param.5, bf16[64,8,2,128]{3,2,1,0:T(2,128)(2,1)S(1)} %bitcast.37), kind=kLoop, calls=%fused_computation.16 | loop fusion | flops 131072 | bytes 786432 | tf_op jit(solution)/shard_map/mul | solution.py:28
  9.3 0.0 all-gather.2.cloned.1.call-update
  9.3 0.7 %convert_element_type.12 = bf16[2,4,2]{1,2,0:T(2,128)(2,1)S(1)} convert(s32[2,4,2]{1,2,0:T(2,128)} %param.8) | non-fusion elementwise | flops 16 | bytes 96 | tf_op jit(solution)/shard_map/convert_element_type | solution.py:28
  10.0 0.0 copy-start.2
  10.0 0.2 mul.47
  10.2 0.2 mul.48
  10.4 0.0 copy-done.1
  10.4 0.2 copy.6
  10.6 0.1 mul.49
  10.8 3.0 %collective-permute-start.1 = (bf16[2,512,256]{1,2,0:T(8,128)(2,1)S(1)}, bf16[2,512,256]{1,2,0:T(8,128)(2,1)S(1)}, u32[]{:S(2)}, u32[]{:S(2)}) collective-permute-start(bf16[2,512,256]{1,2,0:T(8,128)(2,1)S(1)} %mul.49), channel_id=1, source_target_pairs={{0,8},{8,16},{16,24},{24,0},{1,9},{9,17},{17,25},{25,1},{2,10},{10... | collective-permute-start | bytes 1572872 | tf_op jit(solution)/shard_map/ppermute | solution.py:15
  13.8 1.0 %collective-permute-start = (bf16[2,512,256]{1,2,0:T(8,128)(2,1)S(1)}, bf16[2,512,256]{1,2,0:T(8,128)(2,1)S(1)}, u32[]{:S(2)}, u32[]{:S(2)}) collective-permute-start(bf16[2,512,256]{1,2,0:T(8,128)(2,1)S(1)} %mul.49), channel_id=1, source_target_pairs={{0,24},{8,0},{16,8},{24,16},{1,25},{9,1},{17,9},{25,17},{2,26},{10... | collective-permute-start | bytes 1572872 | tf_op jit(solution)/shard_map/ppermute | solution.py:17
  14.8 0.0 copy-done.2
  14.8 0.1 mul.57
  15.0 12.5 %collective-permute-done.1 = bf16[2,512,256]{1,2,0:T(8,128)(2,1)S(1)} collective-permute-done((bf16[2,512,256]{1,2,0:T(8,128)(2,1)S(1)}, bf16[2,512,256]{1,2,0:T(8,128)(2,1)S(1)}, u32[]{:S(2)}, u32[]{:S(2)}) %collective-permute-start.1) | collective-permute-done | bytes 524320 | tf_op jit(solution)/shard_map/ppermute | solution.py:15
  27.5 1.1 %collective-permute-start.2 = (bf16[2,512,256]{1,2,0:T(8,128)(2,1)S(1)}, bf16[2,512,256]{1,2,0:T(8,128)(2,1)S(1)}, u32[]{:S(2)}, u32[]{:S(2)}) collective-permute-start(bf16[2,512,256]{1,2,0:T(8,128)(2,1)S(1)} %collective-permute-done.1), channel_id=1, source_target_pairs={{0,8},{8,16},{16,24},{24,0},{1,9},{9,17},{17,25},{25,1},{2,10},{10... | collective-permute-start | bytes 1572872 | tf_op jit(solution)/shard_map/ppermute | solution.py:15
  28.6 14.2 %all-gather.2.cloned.1.call-done = bf16[512,2048]{1,0:T(8,128)(2,1)} async-done(((bf16[512,256]{1,0:T(8,128)(2,1)}), bf16[512,2048]{1,0:T(8,128)(2,1)}) %all-gather.2.cloned.1.call-update) | async-done | bytes 2097168 | tf_op jit(solution)/shard_map/all_gather | solution.py:36
  42.8 0.0 copy-start
  42.8 1.7 %fusion.6 = f32[2,256,512]{2,1,0:T(8,128)S(1)} fusion(bf16[2,512,256]{1,2,0:T(8,128)(2,1)S(1)} %mul.49, bf16[512,2048]{1,0:T(8,128)(2,1)} %all-gather.2.cloned.1.call-done, s32[]{:T(128)S(6)} %select_n.27), kind=kOutput, calls=%fused_computation.10 | convolution fusion | flops 268435456 | bytes 2097156 | tf_op jit(solution)/shard_map/ik,dkj->dij/dot_general | solution.py:41
  44.5 0.0 collective-permute-done
  44.5 0.1 copy-done
  44.6 0.5 convolution_add_fusion.2
  45.0 0.5 convolution_add_fusion.1
  45.5 3.6 %collective-permute-done.2 = bf16[2,512,256]{1,2,0:T(8,128)(2,1)S(1)} collective-permute-done((bf16[2,512,256]{1,2,0:T(8,128)(2,1)S(1)}, bf16[2,512,256]{1,2,0:T(8,128)(2,1)S(1)}, u32[]{:S(2)}, u32[]{:S(2)}) %collective-permute-start.2) | collective-permute-done | bytes 524320 | tf_op jit(solution)/shard_map/ppermute | solution.py:15
  49.2 0.5 fusion.2
  49.6 1.0 %copy.8 = bf16[2,512,256]{2,1,0:T(8,128)(2,1)} copy(bf16[2,512,256]{1,2,0:T(8,128)(2,1)S(1)} %fusion.2) | data formatting | bytes 1048576 | tf_op jit(solution)/shard_map/convert_element_type | solution.py:48
  (2 shorter events, 0.0 us)
Async XLA Ops:
  6.5 3.9 %copy-start.1 = (bf16[2,512,256]{2,1,0:T(8,128)(2,1)S(1)}, bf16[2,512,256]{2,1,0:T(8,128)(2,1)}, u32[]{:S(2)}) copy-start(bf16[2,512,256]{2,1,0:T(8,128)(2,1)} %param.7) | copy-start | bytes 1572868
  6.5 36.3 %all-gather.2.cloned.1.call-start = ((), (), s32[]{:S(2)}) async-start(), calls=%async_computation | async-start | bytes 2359296 | tf_op jit(solution)/shard_map/all_gather | solution.py:36
  10.0 4.8 %copy-start.2 = (s32[4,2]{0,1:T(2,128)S(1)}, s32[4,2]{0,1:T(2,128)}, u32[]{:S(2)}) copy-start(s32[4,2]{0,1:T(2,128)} %param.9) | copy-start | bytes 100
  10.8 16.7 %collective-permute-start.1 = (bf16[2,512,256]{1,2,0:T(8,128)(2,1)S(1)}, bf16[2,512,256]{1,2,0:T(8,128)(2,1)S(1)}, u32[]{:S(2)}, u32[]{:S(2)}) collective-permute-start(bf16[2,512,256]{1,2,0:T(8,128)(2,1)S(1)} %mul.49), channel_id=1, source_target_pairs={{0,8},{8,16},{16,24},{24,0},{1,9},{9,17},{17,25},{25,1},{2,10},{10... | collective-permute-start | bytes 1572872 | tf_op jit(solution)/shard_map/ppermute | solution.py:15
  13.8 30.7 %collective-permute-start = (bf16[2,512,256]{1,2,0:T(8,128)(2,1)S(1)}, bf16[2,512,256]{1,2,0:T(8,128)(2,1)S(1)}, u32[]{:S(2)}, u32[]{:S(2)}) collective-permute-start(bf16[2,512,256]{1,2,0:T(8,128)(2,1)S(1)} %mul.49), channel_id=1, source_target_pairs={{0,24},{8,0},{16,8},{24,16},{1,25},{9,1},{17,9},{25,17},{2,26},{10... | collective-permute-start | bytes 1572872 | tf_op jit(solution)/shard_map/ppermute | solution.py:17
  27.5 21.6 %collective-permute-start.2 = (bf16[2,512,256]{1,2,0:T(8,128)(2,1)S(1)}, bf16[2,512,256]{1,2,0:T(8,128)(2,1)S(1)}, u32[]{:S(2)}, u32[]{:S(2)}) collective-permute-start(bf16[2,512,256]{1,2,0:T(8,128)(2,1)S(1)} %collective-permute-done.1), channel_id=1, source_target_pairs={{0,8},{8,16},{16,24},{24,0},{1,9},{9,17},{17,25},{25,1},{2,10},{10... | collective-permute-start | bytes 1572872 | tf_op jit(solution)/shard_map/ppermute | solution.py:15
  42.8 1.8 %copy-start = (bf16[512,2048]{1,0:T(8,128)(2,1)S(1)}, bf16[512,2048]{1,0:T(8,128)(2,1)}, u32[]{:S(2)}) copy-start(bf16[512,2048]{1,0:T(8,128)(2,1)} %all-gather.2.cloned.1.call-done) | copy-start | bytes 6291460
Sparse Core Ops, SparseCore 0:
  9.4 33.3 all-gather.1

commit v2 on v0

--- a/solution.py
+++ b/solution.py
@@ -17,7 +17,7 @@
     blocksize = density.shape[1] // density_mask.shape[1]
     masked_density = expand_blocks(density, density_mask, blocksize)
     masked_response = expand_blocks(response, response_mask, blocksize)
-    density_full = lax.all_gather(masked_density, "col", axis=1, tiled=True)
+    density_full = jnp.concatenate(lax.all_gather(masked_density, "col"), axis=1)
     result = jnp.einsum(
         "ik,dkj->dij",
         density_full,

time: 92.2 us -> 89.2 us (0.967)
  the two profiles are of different devices: /device:TPU:9 before, /device:TPU:0 now
where the time goes in v2:
time: 89.2 us; the launch traced here: 89 us
  waiting for transfers between devices  60.7 us (68%)
  between operations  13.5 us (15%)
  local copies, waits for them, and re-layouts  7.23 us (8%)
  other arithmetic  4.07 us (5%)
  matrix products  3.5 us (4%)
    all_gather x1, waiting for transfers between devices, body(): lax.all_gather(masked_response, 'row', axis=1, tiled=True)  31.2 us
    all_gather x1, waiting for transfers between devices, body(): lax.all_gather(masked_density, 'col')  29.5 us
    dot_general x1, matrix products, body(): jnp.einsum('ik,dkj->dij', density_full, lax.all_gather(masked_response, '...  3.5 us
    all_gather x1, local copies, waits for them, and re-layouts, body(): lax.all_gather(masked_density, 'col')  2.76 us
    mul x2, other arithmetic, expand_blocks(): scaled = shaped * mask.astype(values.dtype)[..., :, None, :, None]  2.64 us
    reshape x1, local copies, waits for them, and re-layouts, body(): jnp.concatenate(lax.all_gather(masked_density, 'col'), axis=1)  2.35 us
  transfers between devices with their start and end apart: 2, of which 2 were waited for; matrix products, arithmetic and copies ran while one was open for 8% of the time, Pallas kernels for 0%

profile of v2, /device:TPU:0, one launch (start us, length us, event | category | flops | bytes accessed | tf_op | source)
XLA Modules:
  0.0 89.0 jit_solution(15275198282727554696)
XLA Ops:
  6.5 0.0 copy-start
  6.5 0.0 all-gather.6.cloned.1.call-start
  6.5 0.7 convert_element_type.13
  7.3 0.1 copy.7
  7.4 0.2 mul.41
  7.6 1.7 %bitcast_multiply_fusion = bf16[512,256]{1,0:T(8,128)(2,1)} fusion(bf16[512,256]{1,0:T(8,128)(2,1)} %param.5, bf16[64,8,2,128]{3,2,1,0:T(2,128)(2,1)S(1)} %bitcast.28), kind=kLoop, calls=%fused_computation.5 | loop fusion | flops 131072 | bytes 786432 | tf_op jit(solution)/shard_map/mul | solution.py:12
  9.3 0.0 all-gather.6.cloned.1.call-update
  9.3 0.0 all-gather.4.cloned.1.call-start
  9.4 0.7 convert_element_type.12
  10.1 0.2 mul.38
  10.3 0.0 copy-start.1
  10.3 0.2 mul.39
  10.5 0.0 copy-done
  10.5 0.2 copy.6
  10.7 0.9 %mul.40 = bf16[2,512,256]{1,2,0:T(8,128)(2,1)} multiply(bf16[2,512,256]{1,2,0:T(8,128)(2,1)S(1)} %copy.6, bf16[2,512,256]{1,2,0:T(8,128)(2,1)S(1)} %mul.39) | non-fusion elementwise | flops 262144 | bytes 1572864 | tf_op jit(solution)/shard_map/mul | solution.py:12
  11.7 0.0 all-gather.4.cloned.1.call-update
  11.7 0.0 copy-done.1
  11.7 0.1 mul.45
  11.9 29.5 %all-gather.6.cloned.1.call-done = bf16[4096,256]{1,0:T(8,128)(2,1)} async-done(((bf16[512,256]{1,0:T(8,128)(2,1)}), bf16[4096,256]{1,0:T(8,128)(2,1)}) %all-gather.6.cloned.1.call-update) | async-done | bytes 2097168 | tf_op jit(solution)/shard_map/all_gather | solution.py:20
  41.4 2.8 %copy.15 = bf16[8,512,256]{2,0,1:T(8,128)(2,1)S(1)} copy(bf16[8,512,256]{2,1,0:T(8,128)(2,1)} %bitcast.26) | data formatting | bytes 4194304 | tf_op jit(solution)/shard_map/all_gather | solution.py:20
  44.1 2.3 %reshape.25 = bf16[512,2048,1]{1,0,2:T(8,128)(2,1)} reshape(bf16[512,8,256]{2,1,0:T(8,128)(2,1)S(1)} %bitcast.25) | data formatting | bytes 4194304 | tf_op jit(solution)/shard_map/reshape | solution.py:20
  46.5 31.2 %all-gather.4.cloned.1.call-done = bf16[2,2048,256]{1,2,0:T(8,128)(2,1)} async-done(((bf16[2,512,256]{1,2,0:T(8,128)(2,1)}), bf16[2,2048,256]{1,2,0:T(8,128)(2,1)}) %all-gather.4.cloned.1.call-update) | async-done | bytes 2097168 | tf_op jit(solution)/shard_map/all_gather | solution.py:24
  77.7 3.5 %fusion.1 = bf16[2,512,256]{1,2,0:T(8,128)(2,1)S(1)} fusion(bf16[2,2048,256]{1,2,0:T(8,128)(2,1)} %all-gather.4.cloned.1.call-done, bf16[512,2048,1]{1,0,2:T(8,128)(2,1)} %reshape.25, f32[512,256]{0,1:T(8,128)S(1)} %bitcast.29), kind=kOutput, calls=%fused_computation.3 | convolution fusion | flops 1074266112 | bytes 5242880 | tf_op jit(solution)/shard_map/ik,dkj->dij/dot_general | solution.py:21
  81.2 1.0 %copy.9 = bf16[2,512,256]{2,1,0:T(8,128)(2,1)} copy(bf16[2,512,256]{1,2,0:T(8,128)(2,1)S(1)} %fusion.1) | data formatting | bytes 1048576 | tf_op jit(solution)/shard_map/convert_element_type | solution.py:27
  (2 shorter events, 0.0 us)
Async XLA Ops:
  6.5 4.0 %copy-start = (bf16[2,512,256]{2,1,0:T(8,128)(2,1)S(1)}, bf16[2,512,256]{2,1,0:T(8,128)(2,1)}, u32[]{:S(2)}) copy-start(bf16[2,512,256]{2,1,0:T(8,128)(2,1)} %param.7) | copy-start | bytes 1572868
  6.5 34.8 %all-gather.6.cloned.1.call-start = ((), (), s32[]{:S(2)}) async-start(), calls=%async_computation.1 | async-start | bytes 2359296 | tf_op jit(solution)/shard_map/all_gather | solution.py:20
  9.3 68.3 %all-gather.4.cloned.1.call-start = ((), (), s32[]{:S(2)}) async-start(), calls=%async_computation | async-start | bytes 2621440 | tf_op jit(solution)/shard_map/all_gather | solution.py:24
  10.3 1.4 %copy-start.1 = (s32[4,2]{0,1:T(2,128)S(1)}, s32[4,2]{0,1:T(2,128)}, u32[]{:S(2)}) copy-start(s32[4,2]{0,1:T(2,128)} %param.9) | copy-start | bytes 100
Sparse Core Ops, SparseCore 0:
  9.5 31.8 all-gather.5
  43.2 34.4 all-gather.3
